TPU v7x, 32 devices: a whole 2x2x4 slice. The times are simulated.
32 devices in a mesh: sec: 2 (over y), tp: 4 (over x, core), dp: 4 (over z).
Axes of the slice: x: 2, y: 2, z: 4, core: 2. Of those that a mesh axis runs over, the one named last changes fastest.
Arguments:
- feats: bfloat16 [8, 512, 512], P(('sec', 'dp'), 'tp'), may hold values from -6 to 6
- frame_clip: int32 [8, 32], P(('sec', 'dp')), may hold values from 0 to 3, never falling along the last dimension, each value on 1 to 16 neighbouring positions
- clip_order: int32 [8, 4], P(('sec', 'dp')), may hold values from 0 to 3, each once within a row
- conv_weight: bfloat16 [3, 512, 192], replicated, may hold values from -0.15625 to 0.15625
- embed_weight: bfloat16 [192, 3072], replicated, may hold values from -0.4375 to 0.4375
- wq: bfloat16 [3072, 512], P(('sec', 'dp'), 'tp')
- wk: bfloat16 [3072, 512], P(('sec', 'dp'), 'tp')
- wv: bfloat16 [3072, 512], P(('sec', 'dp'), 'tp'), may hold values from -0.109375 to 0.109375
- q_gain: float32 [4, 128], P('tp'), may hold values from 0.6 to 8, as said below
- k_gain: float32 [4, 128], P('tp'), may hold values from 0.6 to 8, as said below
Outputs:
- attended: bfloat16 [8, 512, 512], P(('sec', 'dp'), 'tp')
Inputs may be any that keep to these rules, and one draw needn't show every extreme that they name: `frame_clip`: clip ids never fall along the frames; every clip has at least one frame and one clip has exactly 16 frames. `clip_order`: each row holds every clip once. `q_gain`: positive. `k_gain`: positive.
All inputs are finite; a program needn't handle non-finite values.
Results may differ from a plain program's by a relative error of at most 0.0084.
Values may be sent and summed in bfloat16 or wider, within the bound.
A program may use at most 64 MiB of HBM per device.

v0:
```python
import jax
import jax.numpy as jnp
from jax import lax
from jax.sharding import PartitionSpec as P

HD = 128
PD = 192
TAPS = 3
VP = 16


def from_behind(value, axis, steps):
    count = lax.axis_size(axis)
    leading, last = (max(0, -steps), min(count, count - steps))
    return lax.ppermute(value, axis, [(source, source + steps) for source in range(leading, last)])


def packing(clip_ids, clip_order):
    frame_count = clip_ids.shape[0]
    clip_count = clip_order.shape[0]
    labels = jnp.arange(clip_count, dtype=jnp.int32)
    lengths = jnp.sum((clip_ids[None, :] == labels[:, None]).astype(jnp.int32), axis=1)
    starts = jnp.cumsum(lengths) - lengths
    picked = clip_order[:, None] == labels[None, :]
    packed_len = jnp.sum(jnp.where(picked, lengths[None, :], 0), axis=1)
    packed_from = jnp.sum(jnp.where(picked, starts[None, :], 0), axis=1)
    place_start = jnp.cumsum(packed_len) - packed_len
    frames = jnp.arange(frame_count, dtype=jnp.int32)
    places = jnp.sum((frames[:, None] >= place_start[None, :]).astype(jnp.int32), axis=1) - 1
    chosen = places[:, None] == labels[None, :]
    source = jnp.sum(jnp.where(chosen, (packed_from - place_start)[None, :], 0), axis=1) + frames
    return (source, places)


def normed(values, gains):
    scale = lax.rsqrt(jnp.mean(values * values, axis=-1, keepdims=True) + 1e-06)
    return (values * scale * gains[None, :]).astype(jnp.bfloat16)


def attend_local(projected, slots, segment, gain_q, gain_k):
    ordered = jnp.take(projected, slots, axis=0)
    query = normed(ordered[:, :HD], gain_q)
    key_rows = normed(ordered[:, HD : 2 * HD], gain_k)
    value_rows = ordered[:, 2 * HD :].astype(jnp.bfloat16)
    total = query.shape[0]
    block = min(total, 512)
    query_blocks = query.reshape(total // block, block, HD)
    segment_blocks = segment.reshape(total // block, block)

    def one_block(inputs):
        query_rows, block_seg = inputs
        scores = jnp.dot(query_rows, key_rows.T, preferred_element_type=jnp.float32) * HD ** (-0.5)
        same_seg = block_seg[:, None] == segment[None, :]
        scores = jnp.where(same_seg, scores, -1e30)
        highest = jnp.max(scores, axis=-1, keepdims=True)
        expo = jnp.where(same_seg, jnp.exp(scores - highest), 0.0)
        probs = (expo / jnp.sum(expo, axis=-1, keepdims=True)).astype(jnp.bfloat16)
        return jnp.dot(probs, value_rows, preferred_element_type=jnp.float32).astype(jnp.bfloat16)

    mixed = lax.map(one_block, (query_blocks, segment_blocks))
    return mixed.reshape(total, HD)


def embed_project(every_latent, embed_weight, w_qkv):
    all_tokens = jnp.dot(every_latent, embed_weight, preferred_element_type=jnp.float32).astype(
        jnp.bfloat16
    )
    return jnp.dot(all_tokens, w_qkv, preferred_element_type=jnp.float32)


def local(feats, frame_clip, clip_order, conv_weight, embed_weight, wq, wk, wv, q_gain, k_gain):
    feature = feats[0]
    row_count = feature.shape[0]
    frames_dev = row_count // VP
    reach = TAPS - 1
    rim_rows = from_behind(feature[row_count - reach * VP :], "tp", 1)
    widened = jnp.concatenate([rim_rows, feature], axis=0)
    clip_ids = frame_clip[0]
    padded = jnp.concatenate([jnp.full((reach,), -1, jnp.int32), clip_ids])
    window = lax.dynamic_slice_in_dim(padded, lax.axis_index("tp") * frames_dev, frames_dev + reach)
    own_ids = window[reach:]
    summed = jnp.zeros((row_count, PD), jnp.float32)
    for delay in range(TAPS):
        first = reach - delay
        earlier = widened[first * VP : (first + frames_dev) * VP]
        in_clip = jnp.repeat(window[first : first + frames_dev] == own_ids, VP)
        contrib = jnp.dot(earlier, conv_weight[delay], preferred_element_type=jnp.float32)
        summed = summed + jnp.where(in_clip[:, None], contrib, 0.0)
    latent = summed.astype(jnp.bfloat16)
    full_q, full_k, full_v = (
        lax.all_gather(wq, ("sec", "dp"), axis=0, tiled=True),
        lax.all_gather(wk, ("sec", "dp"), axis=0, tiled=True),
        lax.all_gather(wv, ("sec", "dp"), axis=0, tiled=True),
    )
    w_qkv = jnp.concatenate([full_q, full_k, full_v], axis=1)
    source, places = packing(clip_ids, clip_order[0])
    slots = (source[:, None] * VP + jnp.arange(VP, dtype=jnp.int32)[None, :]).reshape(-1)
    segment = jnp.repeat(places, VP)
    flat_latent = latent.reshape(row_count * PD // 128, 128)
    every_latent = lax.all_gather(flat_latent, "tp", axis=0, tiled=True).reshape(-1, PD)
    projected = embed_project(every_latent, embed_weight, w_qkv)
    mixed = attend_local(projected, slots, segment, q_gain[0], k_gain[0])
    regrouped = lax.all_to_all(mixed, "tp", split_axis=0, concat_axis=1, tiled=True)
    return regrouped[None]


def solution(mesh):
    return jax.shard_map(
        local,
        mesh=mesh,
        in_specs=(
            P(("sec", "dp"), "tp", None),
            P(("sec", "dp"), None),
            P(("sec", "dp"), None),
            P(),
            P(),
            P(("sec", "dp"), "tp"),
            P(("sec", "dp"), "tp"),
            P(("sec", "dp"), "tp"),
            P("tp", None),
            P("tp", None),
        ),
        out_specs=P(("sec", "dp"), "tp", None),
        check_vma=False,
    )
```

profile of v0, /device:TPU:0, one launch (start us, length us, event | category | flops | bytes accessed | tf_op | source)
XLA Modules:
  0.0 136.3 jit_solution(9821429094563022714)
XLA Ops:
  0.0 0.9 slice_bitcast_fusion
  0.9 2.4 %collective-permute-start = (bf16[32,512]{1,0:T(8,128)(2,1)S(1)}, bf16[32,512]{1,0:T(8,128)(2,1)S(1)}, u32[]{:S(2)}, u32[]{:S(2)}) collective-permute-start(bf16[32,512]{1,0:T(8,128)(2,1)S(1)} %slice_bitcast_fusion), channel_id=1, source_target_pairs={{0,4},{4,8},{8,12},{1,5},{5,9},{9,13},{2,6},{6,10},{10,14},{3,7},{... | collective-permute-start | bytes 98312 | tf_op jit(solution)/shard_map/ppermute | solution.py:15
  3.3 0.8 convert_reduce_fusion.1
  4.0 0.2 reduce-window.16
  4.2 0.9 select_reduce_fusion.1
  5.1 0.2 reduce-window.15
  5.7 34.9 %all_gather.15 = bf16[3072,128]{1,0:T(8,128)(2,1)S(1)} all-gather(bf16[384,128]{1,0:T(8,128)(2,1)} %param.17), channel_id=1, replica_groups=mesh['sec'=2,'tp'=4,'dp'=4] {'sec','dp'}, dimensions={0}, use_global_device_ids=true | all-gather | bytes 884736 | tf_op jit(solution)/shard_map/all_gather | solution.py:93
  40.6 34.3 %all_gather.14 = bf16[3072,128]{1,0:T(8,128)(2,1)S(1)} all-gather(bf16[384,128]{1,0:T(8,128)(2,1)} %param.16), channel_id=1, replica_groups=mesh['sec'=2,'tp'=4,'dp'=4] {'sec','dp'}, dimensions={0}, use_global_device_ids=true | all-gather | bytes 884736 | tf_op jit(solution)/shard_map/all_gather | solution.py:92
  75.0 35.1 %all_gather.13 = bf16[3072,128]{1,0:T(8,128)(2,1)} all-gather(bf16[384,128]{1,0:T(8,128)(2,1)S(1)} %copy-done.2), channel_id=1, replica_groups=mesh['sec'=2,'tp'=4,'dp'=4] {'sec','dp'}, dimensions={0}, use_global_device_ids=true | all-gather | bytes 884736 | tf_op jit(solution)/shard_map/all_gather | solution.py:91
  110.0 1.1 fusion.13
  111.9 1.1 fusion.8
  113.0 1.1 fusion.9
  114.4 5.6 %all_gather.12 = bf16[768,128]{1,0:T(8,128)(2,1)S(1)} all-gather(bf16[192,128]{1,0:T(8,128)(2,1)S(1)} %reshape.156), channel_id=1, replica_groups=mesh['sec'=2,'tp'=4,'dp'=4] {'tp'}, dimensions={0}, use_global_device_ids=true | all-gather | bytes 245760 | tf_op jit(solution)/shard_map/all_gather | solution.py:100
  120.0 0.9 reshape.157
  120.9 3.8 %fusion = f32[512,384]{1,0:T(8,128)S(1)} fusion(bf16[3072,128]{1,0:T(8,128)(2,1)S(1)} %all_gather.15, bf16[3072,128]{1,0:T(8,128)(2,1)S(1)} %all_gather.14, bf16[3072,128]{1,0:T(8,128)(2,1)} %all_gather.13, bf16[512,192]{1,0:T(8,128)(2,1)} %reshape.157, bf16[192,3072]{1,0:T(8,128)(2,1)S(1)} %copy-done), kind=kOutput, calls=%fused_computation.2 | convolution fusion | flops 1820590080 | bytes 4521984 | tf_op jit(solution)/shard_map/dot_general | solution.py:68
  124.7 1.6 %gather_fusion = f32[512,384]{1,0:T(8,128)S(1)} fusion(f32[512,384]{1,0:T(8,128)S(1)} %fusion, s32[1024]{0:T(1024)S(1)} %pad_clamp_fusion), kind=kCustom, calls=%fused_computation | custom fusion | bytes 1574912 | tf_op jit(solution)/shard_map/jit(_take)/gather | solution.py:41
  126.4 0.1 broadcast_select_fusion
  126.5 0.2 multiply_reduce_fusion.1
  126.7 0.3 copy-done.4
  127.0 0.4 fusion.31
  127.5 0.2 fusion.10
  127.7 0.5 convolution_convert_fusion.1
  128.2 7.3 %all_to_all.16 = bf16[4,128,128]{2,1,0:T(8,128)(2,1)S(1)} all-to-all(bf16[4,128,128]{2,1,0:T(8,128)(2,1)S(1)} %bitcast.33), channel_id=1, replica_groups=mesh['sec'=2,'tp'=4,'dp'=4] {'tp'}, dimensions={0} | all-to-all | bytes 262144 | tf_op jit(solution)/shard_map/all_to_all | solution.py:103
  135.6 0.7 broadcast_in_dim.128
  (36 shorter events, 1.5 us)
Async XLA Ops:
  0.0 120.9 %copy-start = (bf16[192,3072]{1,0:T(8,128)(2,1)S(1)}, bf16[192,3072]{1,0:T(8,128)(2,1)}, u32[]{:S(2)}) copy-start(bf16[192,3072]{1,0:T(8,128)(2,1)} %param.14) | copy-start | bytes 3538948
  0.0 75.0 %copy-start.2 = (bf16[384,128]{1,0:T(8,128)(2,1)S(1)}, bf16[384,128]{1,0:T(8,128)(2,1)}, u32[]{:S(2)}) copy-start(bf16[384,128]{1,0:T(8,128)(2,1)} %param.15) | copy-start | bytes 294916
  0.9 111.0 %collective-permute-start = (bf16[32,512]{1,0:T(8,128)(2,1)S(1)}, bf16[32,512]{1,0:T(8,128)(2,1)S(1)}, u32[]{:S(2)}, u32[]{:S(2)}) collective-permute-start(bf16[32,512]{1,0:T(8,128)(2,1)S(1)} %slice_bitcast_fusion), channel_id=1, source_target_pairs={{0,4},{4,8},{8,12},{1,5},{5,9},{9,13},{2,6},{6,10},{10,14},{3,7},{... | collective-permute-start | bytes 98312 | tf_op jit(solution)/shard_map/ppermute | solution.py:15
  5.7 104.3 %copy-start.1 = (bf16[1,128,512]{2,1,0:T(8,128)(2,1)S(1)}, bf16[1,128,512]{2,1,0:T(8,128)(2,1)}, u32[]{:S(2)}) copy-start(bf16[1,128,512]{2,1,0:T(8,128)(2,1)} %param.10) | copy-start | bytes 393220
  40.6 70.6 %copy-start.3 = (s32[1,32]{1,0:T(1,128)S(1)}, s32[1,32]{1,0:T(1,128)}, u32[]{:S(2)}) copy-start(s32[1,32]{1,0:T(1,128)} %param.11) | copy-start | bytes 388
  126.3 0.7 copy-start.4
  126.4 0.7 copy-start.5
where the time goes:
time: 137 us; the launch traced here: 136 us
  blocking collectives  117 us (85%)
  matrix products  8.16 us (6%)
  local copies, waits for them, and re-layouts  5.43 us (4%)
  other arithmetic  2.97 us (2%)
  starting transfers between devices  2.39 us (2%)
    all_gather x1, blocking collectives, local(): lax.all_gather(wq, ('sec', 'dp'), axis=0, tiled=True)  35.1 us
    all_gather x1, blocking collectives, local(): lax.all_gather(wv, ('sec', 'dp'), axis=0, tiled=True)  34.9 us
    all_gather x1, blocking collectives, local(): lax.all_gather(wk, ('sec', 'dp'), axis=0, tiled=True)  34.3 us
    all_to_all x1, blocking collectives, local(): lax.all_to_all(mixed, 'tp', split_axis=0, concat_axis=1, tiled=True)  7.29 us
    all_gather x1, blocking collectives, local(): lax.all_gather(flat_latent, 'tp', axis=0, tiled=True).reshape(-1, PD)  5.6 us
    dot_general x1, matrix products, embed_project(): return jnp.dot(all_tokens, w_qkv, preferred_element_type=jnp.float32)  3.81 us
    dot_general x3, matrix products, local(): jnp.dot(earlier, conv_weight[delay], preferred_element_type=jnp.float32)  3.42 us
  transfers between devices with their start and end apart: 1, of which 0 were waited for; matrix products, arithmetic and copies ran while one was open for 3% of the time, Pallas kernels for 0%

commit v1 on v0

v1 whole, which is shorter than its diff:
```python
import functools
import jax
import jax.numpy as jnp
from jax import lax
from jax.experimental import pallas as pl
from jax.experimental.pallas import tpu as pltpu
from jax.sharding import PartitionSpec as P

HD = 128
VP = 16
MESH = pl.DeviceIdType.MESH
BF16 = jnp.bfloat16
F32 = jnp.float32


def dot32(a, b):
    return jnp.dot(a, b, preferred_element_type=F32)


def kernel(
    sizes, direct_embed,
    frame_ref, order_ref, feats_ref, conv_ref, embed_ref, wq_ref, wk_ref, wv_ref, gq_ref, gk_ref,
    out_ref,
    wide, conv, embed, weights, part_out, part_in, own_sum, left_in, left_out, right_in, right_out,
    latents, queries, keys, values, mixed,
    local_sem, rim_send, rim_recv, sec_send, sec_recv, dp_send, dp_recv, lat_send, lat_recv, out_send, out_recv,
):
    n_sec, n_tp, n_dp = sizes
    sec, me, dp = lax.axis_index("sec"), lax.axis_index("tp"), lax.axis_index("dp")
    rows = feats_ref.shape[0]
    taps, fin, pd = conv_ref.shape
    depth = wq_ref.shape[0]
    reach_rows = (taps - 1) * VP
    total = rows * n_tp
    frame_count = frame_ref.shape[1]
    clip_count = order_ref.shape[1]
    sec_peers = [lax.rem(sec + d, n_sec) for d in range(1, n_sec)]
    tp_peers = [lax.rem(me + d, n_tp) for d in range(1, n_tp)]

    barrier = pltpu.get_barrier_semaphore()

    def greet(where):
        pl.semaphore_signal(barrier, inc=1, device_id=where, device_id_type=MESH)

    for peer in sec_peers:
        greet({"sec": peer})
    for peer in tp_peers:
        greet({"tp": peer})

    @pl.when(dp > 0)
    def _():
        greet({"dp": dp - 1})

    @pl.when(dp < n_dp - 1)
    def _():
        greet({"dp": dp + 1})

    if direct_embed:
        begin = pl.multiple_of((sec * n_dp + dp) * depth, 128)
        embed_from = embed_ref.at[:, pl.ds(begin, depth)]
    else:
        embed_from = embed_ref
    loads = [
        pltpu.make_async_copy(embed_from, embed, local_sem.at[0]),
        pltpu.make_async_copy(wq_ref, weights.at[0], local_sem.at[1]),
        pltpu.make_async_copy(wk_ref, weights.at[1], local_sem.at[2]),
        pltpu.make_async_copy(wv_ref, weights.at[2], local_sem.at[3]),
        pltpu.make_async_copy(feats_ref, wide.at[pl.ds(reach_rows, rows)], local_sem.at[4]),
        pltpu.make_async_copy(conv_ref, conv, local_sem.at[5]),
    ]
    for load in loads:
        load.start()

    first = [jnp.int32(0) for _ in range(clip_count)]
    for f in range(frame_count):
        clip = frame_ref[0, f]
        for c in range(1, clip_count):
            first[c] = first[c] + (clip < c).astype(jnp.int32)
    lengths = [
        (first[c + 1] if c + 1 < clip_count else jnp.int32(frame_count)) - first[c]
        for c in range(clip_count)
    ]
    place_start, place_shift, place_of = [], [], [jnp.int32(0) for _ in range(clip_count)]
    running = jnp.int32(0)
    for r in range(clip_count):
        clip = order_ref[0, r]
        length, start = jnp.int32(0), jnp.int32(0)
        for c in range(clip_count):
            here = clip == c
            length = jnp.where(here, lengths[c], length)
            start = jnp.where(here, first[c], start)
            place_of[c] = jnp.where(here, r, place_of[c])
        place_start.append(running)
        place_shift.append(start - running)
        running = running + length

    def clip_at(row):
        clip = jnp.zeros_like(row)
        for c in range(1, clip_count):
            clip = clip + (row >= first[c] * VP).astype(jnp.int32)
        return clip

    for load in loads[:4]:
        load.wait()
    for c in range(3):
        partial = dot32(embed[...], weights[c])
        own_sum[c] = partial
        part_out[c] = partial.astype(BF16)

    line_peers = (dp > 0).astype(jnp.int32) + (dp < n_dp - 1).astype(jnp.int32)
    pl.semaphore_wait(barrier, (n_sec - 1) + (n_tp - 1) + line_peers)

    def rim_copy():
        return pltpu.make_async_remote_copy(
            src_ref=feats_ref.at[pl.ds(rows - reach_rows, reach_rows)],
            dst_ref=wide.at[pl.ds(0, reach_rows)],
            send_sem=rim_send, recv_sem=rim_recv,
            device_id={"tp": jnp.minimum(me + 1, n_tp - 1)}, device_id_type=MESH,
        )

    @pl.when(me < n_tp - 1)
    def _():
        rim_copy().start()

    sec_copies = []
    for c in range(3):
        for d in range(1, n_sec):
            copy = pltpu.make_async_remote_copy(
                src_ref=part_out.at[c], dst_ref=part_in.at[d - 1, c],
                send_sem=sec_send.at[d - 1, c], recv_sem=sec_recv.at[d - 1, c],
                device_id={"sec": sec_peers[d - 1]}, device_id_type=MESH,
            )
            copy.start()
            sec_copies.append(copy)

    @pl.when(me == 0)
    def _():
        wide[pl.ds(0, reach_rows), :] = jnp.zeros((reach_rows, fin), BF16)

    loads[4].wait()
    loads[5].wait()

    @pl.when(me > 0)
    def _():
        rim_copy().wait_recv()

    row = me * rows + lax.broadcasted_iota(jnp.int32, (rows, 1), 0)
    own_clip = clip_at(row)
    summed = None
    for delay in range(taps):
        contrib = dot32(wide[pl.ds(reach_rows - delay * VP, rows), :], conv[delay])
        if delay:
            before = row - delay * VP
            in_clip = (before >= 0) & (clip_at(before) == own_clip)
            summed = summed + jnp.where(in_clip, contrib, 0.0)
        else:
            summed = contrib
    latents[me] = summed.astype(BF16)
    lat_copies = []
    for d in range(1, n_tp):
        copy = pltpu.make_async_remote_copy(
            src_ref=latents.at[me], dst_ref=latents.at[me],
            send_sem=lat_send.at[d - 1], recv_sem=lat_recv.at[d - 1],
            device_id={"tp": tp_peers[d - 1]}, device_id_type=MESH,
        )
        copy.start()
        lat_copies.append(copy)

    def line_copy(src, dst, way, c, target):
        return pltpu.make_async_remote_copy(
            src_ref=src.at[c], dst_ref=dst.at[c],
            send_sem=dp_send.at[way, c], recv_sem=dp_recv.at[way, c],
            device_id={"dp": jnp.clip(target, 0, n_dp - 1)}, device_id_type=MESH,
        )

    def to_right(c):
        return line_copy(right_out, left_in, 0, c, dp + 1)

    def to_left(c):
        return line_copy(left_out, right_in, 1, c, dp - 1)

    for c in range(3):
        sum_here = own_sum[c]
        for d in range(1, n_sec):
            sec_copies[c * (n_sec - 1) + d - 1].wait_recv()
            sum_here = sum_here + part_in[d - 1, c].astype(F32)
        own_sum[c] = sum_here
        if n_dp > 1:
            @pl.when(dp == 0)
            def _():
                right_out[c] = sum_here.astype(BF16)
                to_right(c).start()

            @pl.when(dp == n_dp - 1)
            def _():
                left_out[c] = sum_here.astype(BF16)
                to_left(c).start()

    def pass_right():
        for c in range(3):
            @pl.when(dp > 0)
            def _():
                to_right(c).wait_recv()

            @pl.when((dp > 0) & (dp < n_dp - 1))
            def _():
                right_out[c] = (own_sum[c] + left_in[c].astype(F32)).astype(BF16)
                to_right(c).start()

    def pass_left():
        for c in range(3):
            @pl.when(dp < n_dp - 1)
            def _():
                to_left(c).wait_recv()

            @pl.when((dp > 0) & (dp < n_dp - 1))
            def _():
                left_out[c] = (own_sum[c] + right_in[c].astype(F32)).astype(BF16)
                to_left(c).start()

    @pl.when(2 * dp < n_dp)
    def _():
        pass_right()

    pass_left()

    @pl.when(2 * dp >= n_dp)
    def _():
        pass_right()

    for copy in lat_copies:
        copy.wait_recv()
    latent = latents[...].reshape(total, pd)

    def projected(c):
        full = own_sum[c]
        if n_dp > 1:
            full = full + jnp.where(dp > 0, left_in[c].astype(F32), 0.0)
            full = full + jnp.where(dp < n_dp - 1, right_in[c].astype(F32), 0.0)
        high = full.astype(BF16)
        low = (full - high.astype(F32)).astype(BF16)
        both = dot32(latent, jnp.concatenate([high, low], axis=1))
        return both[:, :HD] + both[:, HD:]

    def normed(value, gain):
        scale = lax.rsqrt(jnp.mean(value * value, axis=-1, keepdims=True) + 1e-06)
        return (value * scale * gain).astype(BF16)

    queries[...] = normed(projected(0), gq_ref[...])
    keys[...] = normed(projected(1), gk_ref[...])
    values[...] = projected(2).astype(BF16)

    key_row = lax.broadcasted_iota(jnp.int32, (1, total), 1)
    key_clip = clip_at(key_row)
    key_place = jnp.zeros_like(key_clip)
    for c in range(clip_count):
        key_place = jnp.where(key_clip == c, place_of[c], key_place)

    def attend(block):
        token = block * rows + lax.broadcasted_iota(jnp.int32, (rows, 1), 0)
        place = jnp.zeros_like(token)
        shift = jnp.zeros_like(token) + place_shift[0] * VP
        for r in range(1, clip_count):
            here = token >= place_start[r] * VP
            place = place + here.astype(jnp.int32)
            shift = jnp.where(here, place_shift[r] * VP, shift)
        picks = jnp.where(token + shift == key_row, 1.0, 0.0).astype(BF16)
        query = dot32(picks, queries[...]).astype(BF16)
        scores = lax.dot_general(
            query, keys[...], (((1,), (1,)), ((), ())), preferred_element_type=F32
        )
        scores = jnp.where(place == key_place, scores, -1e30)
        highest = jnp.max(scores, axis=-1, keepdims=True)
        expo = jnp.exp((scores - highest) * HD ** (-0.5))
        weight = jnp.sum(expo, axis=-1, keepdims=True)
        return (dot32(expo.astype(BF16), values[...]) / weight).astype(BF16)

    out_copies = []
    for d in sorted(range(1, n_tp), key=lambda d: abs(2 * d - n_tp)):
        peer = tp_peers[d - 1]
        mixed[d - 1] = attend(peer)
        copy = pltpu.make_async_remote_copy(
            src_ref=mixed.at[d - 1], dst_ref=out_ref.at[me],
            send_sem=out_send.at[d - 1], recv_sem=out_recv.at[d - 1],
            device_id={"tp": peer}, device_id_type=MESH,
        )
        copy.start()
        out_copies.append(copy)
    out_ref[me] = attend(me)

    for copy in sec_copies + lat_copies:
        copy.wait_send()

    @pl.when(me < n_tp - 1)
    def _():
        rim_copy().wait_send()

    @pl.when(dp < n_dp - 1)
    def _():
        for c in range(3):
            to_right(c).wait_send()

    @pl.when(dp > 0)
    def _():
        for c in range(3):
            to_left(c).wait_send()

    for copy in out_copies:
        copy.wait()


def local(sizes, feats, frame_clip, clip_order, conv_weight, embed_weight, wq, wk, wv, q_gain, k_gain):
    n_sec, n_tp, n_dp = sizes
    feature = feats[0]
    rows, fin = feature.shape
    taps, _, pd = conv_weight.shape
    depth = wq.shape[0]
    total = rows * n_tp
    direct_embed = depth % 128 == 0
    if not direct_embed:
        slot = lax.axis_index("sec") * n_dp + lax.axis_index("dp")
        embed_weight = lax.dynamic_slice_in_dim(embed_weight, slot * depth, depth, 1)
    hbm, vmem, smem = (
        pl.BlockSpec(memory_space=space) for space in (pl.ANY, pltpu.VMEM, pltpu.SMEM)
    )
    dma = pltpu.SemaphoreType.DMA
    sec_links, tp_links = max(1, n_sec - 1), max(1, n_tp - 1)
    pieces = (3, pd, HD)
    out = pl.pallas_call(
        functools.partial(kernel, sizes, direct_embed),
        out_shape=jax.ShapeDtypeStruct((n_tp, rows, HD), BF16),
        in_specs=[smem, smem, hbm, hbm, hbm, hbm, hbm, hbm, vmem, vmem],
        out_specs=vmem,
        scratch_shapes=[
            pltpu.VMEM(((taps - 1) * VP + rows, fin), BF16),
            pltpu.VMEM(conv_weight.shape, BF16),
            pltpu.VMEM((pd, depth), BF16),
            pltpu.VMEM((3, depth, HD), BF16),
            pltpu.VMEM(pieces, BF16),
            pltpu.VMEM((sec_links,) + pieces, BF16),
            pltpu.VMEM(pieces, F32),
            pltpu.VMEM(pieces, BF16),
            pltpu.VMEM(pieces, BF16),
            pltpu.VMEM(pieces, BF16),
            pltpu.VMEM(pieces, BF16),
            pltpu.VMEM((n_tp, rows, pd), BF16),
            pltpu.VMEM((total, HD), BF16),
            pltpu.VMEM((total, HD), BF16),
            pltpu.VMEM((total, HD), BF16),
            pltpu.VMEM((tp_links, rows, HD), BF16),
            dma((6,)),
            dma(()),
            dma(()),
            dma((sec_links, 3)),
            dma((sec_links, 3)),
            dma((2, 3)),
            dma((2, 3)),
            dma((tp_links,)),
            dma((tp_links,)),
            dma((tp_links,)),
            dma((tp_links,)),
        ],
        compiler_params=pltpu.CompilerParams(collective_id=0, has_side_effects=True),
    )(frame_clip, clip_order, feature, conv_weight, embed_weight, wq, wk, wv, q_gain, k_gain)
    return jnp.transpose(out, (1, 0, 2)).reshape(1, rows, n_tp * HD)


def solution(mesh):
    sizes = tuple(mesh.shape[name] for name in ("sec", "tp", "dp"))
    return jax.shard_map(
        functools.partial(local, sizes),
        mesh=mesh,
        in_specs=(
            P(("sec", "dp"), "tp", None),
            P(("sec", "dp"), None),
            P(("sec", "dp"), None),
            P(),
            P(),
            P(("sec", "dp"), "tp"),
            P(("sec", "dp"), "tp"),
            P(("sec", "dp"), "tp"),
            P("tp", None),
            P("tp", None),
        ),
        out_specs=P(("sec", "dp"), "tp", None),
        check_vma=False,
    )
```

time: 137 us -> 30 us (0.22)
  the two profiles are of different devices: /device:TPU:0 before, /device:TPU:1 now
where the time goes in v1:
time: 30 us; the launch traced here: 29.8 us
  Pallas kernels  25.8 us (86%)
  local copies, waits for them, and re-layouts  4.01 us (13%)
    pallas_call x1, Pallas kernels, local(): pl.pallas_call(functools.partial(kernel, sizes, direct_embed), out_shape=...  25.8 us
    unnamed x1, local copies, waits for them, and re-layouts  2.21 us
    transpose x1, local copies, waits for them, and re-layouts, local(): return jnp.transpose(out, (1, 0, 2)).reshape(1, rows, n_tp * HD)  1.02 us
    reshape x1, local copies, waits for them, and re-layouts, local(): return jnp.transpose(out, (1, 0, 2)).reshape(1, rows, n_tp * HD)  0.77 us

profile of v1, /device:TPU:1, one launch (start us, length us, event | category | flops | bytes accessed | tf_op | source)
XLA Modules:
  0.0 29.8 jit_solution(16613313760804159960)
XLA Ops:
  0.0 2.2 %copy.12.conv_ref = bf16[3,512,192]{2,1,0:T(8,128)(2,1)} copy(bf16[3,512,192]{1,2,0:T(8,128)(2,1)} %param.13) | data formatting | bytes 1179648 | tf_op args[3]
  2.2 25.8 %shard_map.100 = bf16[4,128,128]{2,1,0:T(8,128)(2,1)} custom-call(s32[1,32]{1,0:T(1,128)} %frame_ref.1, s32[1,4]{1,0:T(1,128)} %order_ref.1, bf16[128,512]{1,0:T(8,128)(2,1)} %bitcast.5, bf16[3,512,192]{2,1,0:T(8,128)(2,1)} %copy.12.conv_ref, bf16[192,3072]{1,0:T(8,128)(2,1)} %embed_ref.1, bf16[384,128]{1,0:T(8,128)(2,1)} %wq_ref.1, ...), custom_call_target="tpu_custom_call" | custom-call | tf_op jit(solution)/shard_map/pallas_call | solution.py:329
  28.0 1.0 %copy.13 = bf16[128,4,128]{0,2,1:T(8,128)(2,1)S(1)} copy(bf16[128,4,128]{2,0,1:T(8,128)(2,1)} %bitcast.3) | data formatting | bytes 262144 | tf_op jit(solution)/shard_map/transpose | solution.py:365
  29.1 0.8 %copy.14 = bf16[1,128,512]{2,1,0:T(8,128)(2,1)} copy(bf16[1,128,512]{1,2,0:T(8,128)(2,1)S(1)} %bitcast.4) | data formatting | bytes 262144 | tf_op jit(solution)/shard_map/reshape | solution.py:365

commit v2 on v1

--- a/solution.py
+++ b/solution.py
@@ -17,25 +17,40 @@
     return jnp.dot(a, b, preferred_element_type=F32)
 
 
+def dot_t(a, b):
+    return lax.dot_general(a, b, (((1,), (1,)), ((), ())), preferred_element_type=F32)
+
+
+def partner(index, step, count):
+    if count & (count - 1):
+        return lax.rem(index + step, count)
+    peer, weight = 0, 1
+    while weight < count:
+        bit = lax.rem(lax.div(index, weight), 2)
+        peer = peer + weight * (1 - bit if step & weight else bit)
+        weight *= 2
+    return peer
+
+
 def kernel(
     sizes, direct_embed,
     frame_ref, order_ref, feats_ref, conv_ref, embed_ref, wq_ref, wk_ref, wv_ref, gq_ref, gk_ref,
     out_ref,
-    wide, conv, embed, weights, part_out, part_in, own_sum, left_in, left_out, right_in, right_out,
+    wide, conv, embed, weights, own_sum, sec_out, sec_in, left_in, left_out, right_in, right_out,
     latents, queries, keys, values, mixed,
     local_sem, rim_send, rim_recv, sec_send, sec_recv, dp_send, dp_recv, lat_send, lat_recv, out_send, out_recv,
 ):
     n_sec, n_tp, n_dp = sizes
     sec, me, dp = lax.axis_index("sec"), lax.axis_index("tp"), lax.axis_index("dp")
     rows = feats_ref.shape[0]
-    taps, fin, pd = conv_ref.shape
+    taps, pd, fin = conv_ref.shape
     depth = wq_ref.shape[0]
     reach_rows = (taps - 1) * VP
     total = rows * n_tp
     frame_count = frame_ref.shape[1]
     clip_count = order_ref.shape[1]
     sec_peers = [lax.rem(sec + d, n_sec) for d in range(1, n_sec)]
-    tp_peers = [lax.rem(me + d, n_tp) for d in range(1, n_tp)]
+    tp_peers = [partner(me, d, n_tp) for d in range(1, n_tp)]
 
     barrier = pltpu.get_barrier_semaphore()
 
@@ -100,13 +115,6 @@
             clip = clip + (row >= first[c] * VP).astype(jnp.int32)
         return clip
 
-    for load in loads[:4]:
-        load.wait()
-    for c in range(3):
-        partial = dot32(embed[...], weights[c])
-        own_sum[c] = partial
-        part_out[c] = partial.astype(BF16)
-
     line_peers = (dp > 0).astype(jnp.int32) + (dp < n_dp - 1).astype(jnp.int32)
     pl.semaphore_wait(barrier, (n_sec - 1) + (n_tp - 1) + line_peers)
 
@@ -122,20 +130,95 @@
     def _():
         rim_copy().start()
 
-    sec_copies = []
+    @pl.when(me == 0)
+    def _():
+        wide[pl.ds(0, reach_rows), :] = jnp.zeros((reach_rows, fin), BF16)
+
+    def sec_copy(half, c, d):
+        return pltpu.make_async_remote_copy(
+            src_ref=sec_out.at[half, c], dst_ref=sec_in.at[d - 1, half, c],
+            send_sem=sec_send.at[d - 1, half, c], recv_sem=sec_recv.at[d - 1, half, c],
+            device_id={"sec": sec_peers[d - 1]}, device_id_type=MESH,
+        )
+
+    def send_sec(half, c):
+        for d in range(1, n_sec):
+            sec_copy(half, c, d).start()
+
+    def add_sec(half, c):
+        sum_here = own_sum[half, c]
+        for d in range(1, n_sec):
+            sec_copy(half, c, d).wait_recv()
+            sum_here = sum_here + sec_in[d - 1, half, c].astype(F32)
+        return sum_here
+
+    def line_copy(src, dst, way, half, c, target):
+        return pltpu.make_async_remote_copy(
+            src_ref=src.at[half, c], dst_ref=dst.at[half, c],
+            send_sem=dp_send.at[way, half, c], recv_sem=dp_recv.at[way, half, c],
+            device_id={"dp": jnp.clip(target, 0, n_dp - 1)}, device_id_type=MESH,
+        )
+
+    def to_right(half, c):
+        return line_copy(right_out, left_in, 0, half, c, dp + 1)
+
+    def to_left(half, c):
+        return line_copy(left_out, right_in, 1, half, c, dp - 1)
+
+    def begin_line(half, c, value):
+        if n_dp > 1:
+            @pl.when(dp == 0)
+            def _():
+                right_out[half, c] = value
+                to_right(half, c).start()
+
+            @pl.when(dp == n_dp - 1)
+            def _():
+                left_out[half, c] = value
+                to_left(half, c).start()
+
+    def pass_right(half):
+        for c in range(3):
+            @pl.when(dp > 0)
+            def _():
+                to_right(half, c).wait_recv()
+
+            @pl.when((dp > 0) & (dp < n_dp - 1))
+            def _():
+                right_out[half, c] = (own_sum[half, c] + left_in[half, c].astype(F32)).astype(BF16)
+                to_right(half, c).start()
+
+    def pass_left(half):
+        for c in range(3):
+            @pl.when(dp < n_dp - 1)
+            def _():
+                to_left(half, c).wait_recv()
+
+            @pl.when((dp > 0) & (dp < n_dp - 1))
+            def _():
+                left_out[half, c] = (own_sum[half, c] + right_in[half, c].astype(F32)).astype(BF16)
+                to_left(half, c).start()
+
+    def line_sum(half, c):
+        full = own_sum[half, c]
+        if n_dp > 1:
+            full = full + jnp.where(dp > 0, left_in[half, c].astype(F32), 0.0)
+            full = full + jnp.where(dp < n_dp - 1, right_in[half, c].astype(F32), 0.0)
+        return full
+
+    half_rows = pd // 2
+    loads[0].wait()
     for c in range(3):
-        for d in range(1, n_sec):
-            copy = pltpu.make_async_remote_copy(
-                src_ref=part_out.at[c], dst_ref=part_in.at[d - 1, c],
-                send_sem=sec_send.at[d - 1, c], recv_sem=sec_recv.at[d - 1, c],
-                device_id={"sec": sec_peers[d - 1]}, device_id_type=MESH,
-            )
-            copy.start()
-            sec_copies.append(copy)
-
-    @pl.when(me == 0)
-    def _():
-        wide[pl.ds(0, reach_rows), :] = jnp.zeros((reach_rows, fin), BF16)
+        loads[1 + c].wait()
+        partial = dot32(embed[...], weights[c])
+        for half in range(2):
+            piece = partial[half * half_rows : (half + 1) * half_rows]
+            own_sum[half, c] = piece
+            if half == 0:
+                sec_out[0, c] = piece.astype(BF16)
+                send_sec(0, c)
+            else:
+                begin_line(1, c, piece.astype(BF16))
 
     loads[4].wait()
     loads[5].wait()
@@ -148,7 +231,7 @@
     own_clip = clip_at(row)
     summed = None
     for delay in range(taps):
-        contrib = dot32(wide[pl.ds(reach_rows - delay * VP, rows), :], conv[delay])
+        contrib = dot_t(wide[pl.ds(reach_rows - delay * VP, rows), :], conv[delay])
         if delay:
             before = row - delay * VP
             in_clip = (before >= 0) & (clip_at(before) == own_clip)
@@ -157,7 +240,7 @@
             summed = contrib
     latents[me] = summed.astype(BF16)
     lat_copies = []
-    for d in range(1, n_tp):
+    for d in range(n_tp - 1, 0, -1):
         copy = pltpu.make_async_remote_copy(
             src_ref=latents.at[me], dst_ref=latents.at[me],
             send_sem=lat_send.at[d - 1], recv_sem=lat_recv.at[d - 1],
@@ -166,77 +249,43 @@
         copy.start()
         lat_copies.append(copy)
 
-    def line_copy(src, dst, way, c, target):
-        return pltpu.make_async_remote_copy(
-            src_ref=src.at[c], dst_ref=dst.at[c],
-            send_sem=dp_send.at[way, c], recv_sem=dp_recv.at[way, c],
-            device_id={"dp": jnp.clip(target, 0, n_dp - 1)}, device_id_type=MESH,
-        )
-
-    def to_right(c):
-        return line_copy(right_out, left_in, 0, c, dp + 1)
-
-    def to_left(c):
-        return line_copy(left_out, right_in, 1, c, dp - 1)
-
     for c in range(3):
-        sum_here = own_sum[c]
-        for d in range(1, n_sec):
-            sec_copies[c * (n_sec - 1) + d - 1].wait_recv()
-            sum_here = sum_here + part_in[d - 1, c].astype(F32)
-        own_sum[c] = sum_here
-        if n_dp > 1:
-            @pl.when(dp == 0)
-            def _():
-                right_out[c] = sum_here.astype(BF16)
-                to_right(c).start()
-
-            @pl.when(dp == n_dp - 1)
-            def _():
-                left_out[c] = sum_here.astype(BF16)
-                to_left(c).start()
-
-    def pass_right():
-        for c in range(3):
-            @pl.when(dp > 0)
-            def _():
-                to_right(c).wait_recv()
-
-            @pl.when((dp > 0) & (dp < n_dp - 1))
-            def _():
-                right_out[c] = (own_sum[c] + left_in[c].astype(F32)).astype(BF16)
-                to_right(c).start()
-
-    def pass_left():
-        for c in range(3):
-            @pl.when(dp < n_dp - 1)
-            def _():
-                to_left(c).wait_recv()
-
-            @pl.when((dp > 0) & (dp < n_dp - 1))
-            def _():
-                left_out[c] = (own_sum[c] + right_in[c].astype(F32)).astype(BF16)
-                to_left(c).start()
+        sum_here = add_sec(0, c)
+        own_sum[0, c] = sum_here
+        begin_line(0, c, sum_here.astype(BF16))
 
     @pl.when(2 * dp < n_dp)
     def _():
-        pass_right()
-
-    pass_left()
+        pass_right(1)
+        pass_right(0)
+        pass_left(1)
 
     @pl.when(2 * dp >= n_dp)
     def _():
-        pass_right()
+        pass_left(1)
+        pass_left(0)
+        pass_right(1)
+
+    for c in range(3):
+        sum_here = line_sum(1, c)
+        own_sum[1, c] = sum_here
+        sec_out[1, c] = sum_here.astype(BF16)
+        send_sec(1, c)
+
+    @pl.when(2 * dp < n_dp)
+    def _():
+        pass_left(0)
+
+    @pl.when(2 * dp >= n_dp)
+    def _():
+        pass_right(0)
 
     for copy in lat_copies:
         copy.wait_recv()
     latent = latents[...].reshape(total, pd)
 
     def projected(c):
-        full = own_sum[c]
-        if n_dp > 1:
-            full = full + jnp.where(dp > 0, left_in[c].astype(F32), 0.0)
-            full = full + jnp.where(dp < n_dp - 1, right_in[c].astype(F32), 0.0)
+        full = jnp.concatenate([line_sum(0, c), add_sec(1, c)], axis=0)
         high = full.astype(BF16)
         low = (full - high.astype(F32)).astype(BF16)
         both = dot32(latent, jnp.concatenate([high, low], axis=1))
@@ -266,30 +315,35 @@
             shift = jnp.where(here, place_shift[r] * VP, shift)
         picks = jnp.where(token + shift == key_row, 1.0, 0.0).astype(BF16)
         query = dot32(picks, queries[...]).astype(BF16)
-        scores = lax.dot_general(
-            query, keys[...], (((1,), (1,)), ((), ())), preferred_element_type=F32
-        )
+        scores = dot_t(query, keys[...])
         scores = jnp.where(place == key_place, scores, -1e30)
         highest = jnp.max(scores, axis=-1, keepdims=True)
         expo = jnp.exp((scores - highest) * HD ** (-0.5))
         weight = jnp.sum(expo, axis=-1, keepdims=True)
         return (dot32(expo.astype(BF16), values[...]) / weight).astype(BF16)
 
+    def columns(head):
+        return pl.ds(pl.multiple_of(head * HD, HD), HD)
+
     out_copies = []
-    for d in sorted(range(1, n_tp), key=lambda d: abs(2 * d - n_tp)):
+    for d in range(n_tp - 1, 0, -1):
         peer = tp_peers[d - 1]
         mixed[d - 1] = attend(peer)
         copy = pltpu.make_async_remote_copy(
-            src_ref=mixed.at[d - 1], dst_ref=out_ref.at[me],
+            src_ref=mixed.at[d - 1], dst_ref=out_ref.at[:, columns(me)],
             send_sem=out_send.at[d - 1], recv_sem=out_recv.at[d - 1],
             device_id={"tp": peer}, device_id_type=MESH,
         )
         copy.start()
         out_copies.append(copy)
-    out_ref[me] = attend(me)
-
-    for copy in sec_copies + lat_copies:
+    out_ref[:, columns(me)] = attend(me)
+
+    for copy in lat_copies:
         copy.wait_send()
+    for half in range(2):
+        for c in range(3):
+            for d in range(1, n_sec):
+                sec_copy(half, c, d).wait_send()
 
     @pl.when(me < n_tp - 1)
     def _():
@@ -297,13 +351,15 @@
 
     @pl.when(dp < n_dp - 1)
     def _():
-        for c in range(3):
-            to_right(c).wait_send()
+        for half in range(2):
+            for c in range(3):
+                to_right(half, c).wait_send()
 
     @pl.when(dp > 0)
     def _():
-        for c in range(3):
-            to_left(c).wait_send()
+        for half in range(2):
+            for c in range(3):
+                to_left(half, c).wait_send()
 
     for copy in out_copies:
         copy.wait()
@@ -313,7 +369,8 @@
     n_sec, n_tp, n_dp = sizes
     feature = feats[0]
     rows, fin = feature.shape
-    taps, _, pd = conv_weight.shape
+    conv_weight = jnp.swapaxes(conv_weight, 1, 2)
+    taps, pd, _ = conv_weight.shape
     depth = wq.shape[0]
     total = rows * n_tp
     direct_embed = depth % 128 == 0
@@ -325,10 +382,10 @@
     )
     dma = pltpu.SemaphoreType.DMA
     sec_links, tp_links = max(1, n_sec - 1), max(1, n_tp - 1)
-    pieces = (3, pd, HD)
+    pieces = (2, 3, pd // 2, HD)
     out = pl.pallas_call(
         functools.partial(kernel, sizes, direct_embed),
-        out_shape=jax.ShapeDtypeStruct((n_tp, rows, HD), BF16),
+        out_shape=jax.ShapeDtypeStruct((rows, n_tp * HD), BF16),
         in_specs=[smem, smem, hbm, hbm, hbm, hbm, hbm, hbm, vmem, vmem],
         out_specs=vmem,
         scratch_shapes=[
@@ -336,9 +393,9 @@
             pltpu.VMEM(conv_weight.shape, BF16),
             pltpu.VMEM((pd, depth), BF16),
             pltpu.VMEM((3, depth, HD), BF16),
+            pltpu.VMEM(pieces, F32),
             pltpu.VMEM(pieces, BF16),
             pltpu.VMEM((sec_links,) + pieces, BF16),
-            pltpu.VMEM(pieces, F32),
             pltpu.VMEM(pieces, BF16),
             pltpu.VMEM(pieces, BF16),
             pltpu.VMEM(pieces, BF16),
@@ -351,10 +408,10 @@
             dma((6,)),
             dma(()),
             dma(()),
-            dma((sec_links, 3)),
-            dma((sec_links, 3)),
-            dma((2, 3)),
-            dma((2, 3)),
+            dma((sec_links, 2, 3)),
+            dma((sec_links, 2, 3)),
+            dma((2, 2, 3)),
+            dma((2, 2, 3)),
             dma((tp_links,)),
             dma((tp_links,)),
             dma((tp_links,)),
@@ -362,7 +419,7 @@
         ],
         compiler_params=pltpu.CompilerParams(collective_id=0, has_side_effects=True),
     )(frame_clip, clip_order, feature, conv_weight, embed_weight, wq, wk, wv, q_gain, k_gain)
-    return jnp.transpose(out, (1, 0, 2)).reshape(1, rows, n_tp * HD)
+    return out[None]
 
 
 def solution(mesh):

time: 30 us -> 26.2 us (0.87)
  the two profiles are of different devices: /device:TPU:1 before, /device:TPU:0 now
where the time goes in v2:
time: 26.2 us; the launch traced here: 26.1 us
  Pallas kernels  24.5 us (94%)
  local copies, waits for them, and re-layouts  1.57 us (6%)
    pallas_call x1, Pallas kernels, local(): pl.pallas_call(functools.partial(kernel, sizes, direct_embed), out_shape=...  24.5 us
    unnamed x1, local copies, waits for them, and re-layouts  1.57 us

profile of v2, /device:TPU:0, one launch (start us, length us, event | category | flops | bytes accessed | tf_op | source)
XLA Modules:
  0.0 26.1 jit_solution(7814528654242114540)
XLA Ops:
  0.0 24.5 %shard_map.100 = bf16[128,512]{1,0:T(8,128)(2,1)} custom-call(s32[1,32]{1,0:T(1,128)} %frame_ref.1, s32[1,4]{1,0:T(1,128)} %order_ref.1, bf16[128,512]{1,0:T(8,128)(2,1)} %bitcast.5, bf16[3,192,512]{2,1,0:T(8,128)(2,1)} %bitcast.3, bf16[192,3072]{1,0:T(8,128)(2,1)} %embed_ref.1, bf16[384,128]{1,0:T(8,128)(2,1)} %wq_ref.1, bf16[384,128]{1,0:T(8,128)(2,1)} %wk_ref.1, ...), custom_call_target="tpu_custom_call" | custom-call | tf_op jit(solution)/shard_map/pallas_call | solution.py:386
  24.5 1.6 %copy.12 = bf16[1,128,512]{2,1,0:T(8,128)(2,1)} copy(bf16[1,128,512]{2,1,0:T(8,128)(2,1)} %bitcast.4) | data formatting | bytes 262144

commit v3 on v2

--- a/solution.py
+++ b/solution.py
@@ -177,27 +177,25 @@
                 left_out[half, c] = value
                 to_left(half, c).start()
 
-    def pass_right(half):
-        for c in range(3):
-            @pl.when(dp > 0)
-            def _():
-                to_right(half, c).wait_recv()
-
-            @pl.when((dp > 0) & (dp < n_dp - 1))
-            def _():
-                right_out[half, c] = (own_sum[half, c] + left_in[half, c].astype(F32)).astype(BF16)
-                to_right(half, c).start()
-
-    def pass_left(half):
-        for c in range(3):
-            @pl.when(dp < n_dp - 1)
-            def _():
-                to_left(half, c).wait_recv()
-
-            @pl.when((dp > 0) & (dp < n_dp - 1))
-            def _():
-                left_out[half, c] = (own_sum[half, c] + right_in[half, c].astype(F32)).astype(BF16)
-                to_left(half, c).start()
+    def pass_right(half, c):
+        @pl.when(dp > 0)
+        def _():
+            to_right(half, c).wait_recv()
+
+        @pl.when((dp > 0) & (dp < n_dp - 1))
+        def _():
+            right_out[half, c] = (own_sum[half, c] + left_in[half, c].astype(F32)).astype(BF16)
+            to_right(half, c).start()
+
+    def pass_left(half, c):
+        @pl.when(dp < n_dp - 1)
+        def _():
+            to_left(half, c).wait_recv()
+
+        @pl.when((dp > 0) & (dp < n_dp - 1))
+        def _():
+            left_out[half, c] = (own_sum[half, c] + right_in[half, c].astype(F32)).astype(BF16)
+            to_left(half, c).start()
 
     def line_sum(half, c):
         full = own_sum[half, c]
@@ -254,31 +252,44 @@
         own_sum[0, c] = sum_here
         begin_line(0, c, sum_here.astype(BF16))
 
-    @pl.when(2 * dp < n_dp)
-    def _():
-        pass_right(1)
-        pass_right(0)
-        pass_left(1)
-
-    @pl.when(2 * dp >= n_dp)
-    def _():
-        pass_left(1)
-        pass_left(0)
-        pass_right(1)
+        @pl.when(2 * dp < n_dp)
+        def _():
+            pass_right(1, c)
+
+        @pl.when(2 * dp >= n_dp)
+        def _():
+            pass_left(1, c)
 
     for c in range(3):
+        @pl.when(2 * dp < n_dp)
+        def _():
+            pass_left(1, c)
+
+        @pl.when(2 * dp >= n_dp)
+        def _():
+            pass_right(1, c)
+
         sum_here = line_sum(1, c)
         own_sum[1, c] = sum_here
         sec_out[1, c] = sum_here.astype(BF16)
         send_sec(1, c)
 
-    @pl.when(2 * dp < n_dp)
-    def _():
-        pass_left(0)
-
-    @pl.when(2 * dp >= n_dp)
-    def _():
-        pass_right(0)
+        @pl.when(2 * dp < n_dp)
+        def _():
+            pass_right(0, c)
+
+        @pl.when(2 * dp >= n_dp)
+        def _():
+            pass_left(0, c)
+
+    for c in range(3):
+        @pl.when(2 * dp < n_dp)
+        def _():
+            pass_left(0, c)
+
+        @pl.when(2 * dp >= n_dp)
+        def _():
+            pass_right(0, c)
 
     for copy in lat_copies:
         copy.wait_recv()
@@ -385,7 +396,7 @@
     pieces = (2, 3, pd // 2, HD)
     out = pl.pallas_call(
         functools.partial(kernel, sizes, direct_embed),
-        out_shape=jax.ShapeDtypeStruct((rows, n_tp * HD), BF16),
+        out_shape=pltpu.VMEM((rows, n_tp * HD), BF16),
         in_specs=[smem, smem, hbm, hbm, hbm, hbm, hbm, hbm, vmem, vmem],
         out_specs=vmem,
         scratch_shapes=[

time: 26.2 us -> 24 us (0.916)
  Pallas kernels: 24.5 us -> 23.2 us
  local copies, waits for them, and re-layouts: 1.57 us -> 0.66 us
    pallas_call x1, Pallas kernels: 24.5 us -> 23.2 us  [local(): pl.pallas_call(functools.partial(kernel, sizes, direct_embed), out_shape=...]
    unnamed x1, local copies, waits for them, and re-layouts: 1.57 us -> 0.66 us
where the time goes in v3:
time: 24 us; the launch traced here: 23.8 us
  Pallas kernels  23.2 us (97%)
  local copies, waits for them, and re-layouts  0.66 us (3%)
    pallas_call x1, Pallas kernels, local(): pl.pallas_call(functools.partial(kernel, sizes, direct_embed), out_shape=...  23.2 us
    unnamed x1, local copies, waits for them, and re-layouts  0.66 us

profile of v3, /device:TPU:0, one launch (start us, length us, event | category | flops | bytes accessed | tf_op | source)
XLA Modules:
  0.0 23.8 jit_solution(12046408022050604886)
XLA Ops:
  0.0 23.2 %shard_map.100 = bf16[128,512]{1,0:T(8,128)(2,1)S(1)} custom-call(s32[1,32]{1,0:T(1,128)} %frame_ref.1, s32[1,4]{1,0:T(1,128)} %order_ref.1, bf16[128,512]{1,0:T(8,128)(2,1)} %bitcast.5, bf16[3,192,512]{2,1,0:T(8,128)(2,1)} %bitcast.4, bf16[192,3072]{1,0:T(8,128)(2,1)} %embed_ref.1, bf16[384,128]{1,0:T(8,128)(2,1)} %wq_ref.1, bf16[384,128]{1,0:T(8,128)(2,1)} %wk_ref.1, ...), custom_call_target="tpu_custom_call" | custom-call | tf_op jit(solution)/shard_map/pallas_call | solution.py:397
  23.2 0.7 %copy.12 = bf16[1,128,512]{2,1,0:T(8,128)(2,1)} copy(bf16[1,128,512]{2,1,0:T(8,128)(2,1)S(1)} %bitcast.3) | data formatting | bytes 262144

commit v4 on v3

--- a/solution.py
+++ b/solution.py
@@ -34,10 +34,10 @@
 
 def kernel(
     sizes, direct_embed,
-    frame_ref, order_ref, feats_ref, conv_ref, embed_ref, wq_ref, wk_ref, wv_ref, gq_ref, gk_ref,
+    frame_from, order_from, feats_ref, conv_ref, embed_ref, wq_ref, wk_ref, wv_ref, gq_from, gk_from,
     out_ref,
     wide, conv, embed, weights, own_sum, sec_out, sec_in, left_in, left_out, right_in, right_out,
-    latents, queries, keys, values, mixed,
+    latents, packed, queries, keys, values, mixed, frame_ref, order_ref, gq_ref, gk_ref,
     local_sem, rim_send, rim_recv, sec_send, sec_recv, dp_send, dp_recv, lat_send, lat_recv, out_send, out_recv,
 ):
     n_sec, n_tp, n_dp = sizes
@@ -82,38 +82,13 @@
         pltpu.make_async_copy(wv_ref, weights.at[2], local_sem.at[3]),
         pltpu.make_async_copy(feats_ref, wide.at[pl.ds(reach_rows, rows)], local_sem.at[4]),
         pltpu.make_async_copy(conv_ref, conv, local_sem.at[5]),
+        pltpu.make_async_copy(frame_from, frame_ref, local_sem.at[6]),
+        pltpu.make_async_copy(order_from, order_ref, local_sem.at[7]),
+        pltpu.make_async_copy(gq_from, gq_ref, local_sem.at[8]),
+        pltpu.make_async_copy(gk_from, gk_ref, local_sem.at[9]),
     ]
     for load in loads:
         load.start()
-
-    first = [jnp.int32(0) for _ in range(clip_count)]
-    for f in range(frame_count):
-        clip = frame_ref[0, f]
-        for c in range(1, clip_count):
-            first[c] = first[c] + (clip < c).astype(jnp.int32)
-    lengths = [
-        (first[c + 1] if c + 1 < clip_count else jnp.int32(frame_count)) - first[c]
-        for c in range(clip_count)
-    ]
-    place_start, place_shift, place_of = [], [], [jnp.int32(0) for _ in range(clip_count)]
-    running = jnp.int32(0)
-    for r in range(clip_count):
-        clip = order_ref[0, r]
-        length, start = jnp.int32(0), jnp.int32(0)
-        for c in range(clip_count):
-            here = clip == c
-            length = jnp.where(here, lengths[c], length)
-            start = jnp.where(here, first[c], start)
-            place_of[c] = jnp.where(here, r, place_of[c])
-        place_start.append(running)
-        place_shift.append(start - running)
-        running = running + length
-
-    def clip_at(row):
-        clip = jnp.zeros_like(row)
-        for c in range(1, clip_count):
-            clip = clip + (row >= first[c] * VP).astype(jnp.int32)
-        return clip
 
     line_peers = (dp > 0).astype(jnp.int32) + (dp < n_dp - 1).astype(jnp.int32)
     pl.semaphore_wait(barrier, (n_sec - 1) + (n_tp - 1) + line_peers)
@@ -218,8 +193,37 @@
             else:
                 begin_line(1, c, piece.astype(BF16))
 
-    loads[4].wait()
-    loads[5].wait()
+    for load in loads[4:]:
+        load.wait()
+
+    first = [jnp.int32(0) for _ in range(clip_count)]
+    for f in range(frame_count):
+        clip = frame_ref[0, f]
+        for c in range(1, clip_count):
+            first[c] = first[c] + (clip < c).astype(jnp.int32)
+    lengths = [
+        (first[c + 1] if c + 1 < clip_count else jnp.int32(frame_count)) - first[c]
+        for c in range(clip_count)
+    ]
+    place_start, place_shift = [], []
+    running = jnp.int32(0)
+    for r in range(clip_count):
+        clip = order_ref[0, r]
+        length, start = jnp.int32(0), jnp.int32(0)
+        for c in range(clip_count):
+            here = clip == c
+            length = jnp.where(here, lengths[c], length)
+            start = jnp.where(here, first[c], start)
+        place_start.append(running)
+        place_shift.append(start - running)
+        running = running + length
+
+    def clip_at(row):
+        clip = jnp.zeros_like(row)
+        for c in range(1, clip_count):
+            clip = clip + (row >= first[c] * VP).astype(jnp.int32)
+        return clip
+
 
     @pl.when(me > 0)
     def _():
@@ -282,24 +286,45 @@
         def _():
             pass_left(0, c)
 
-    for c in range(3):
-        @pl.when(2 * dp < n_dp)
-        def _():
-            pass_left(0, c)
-
-        @pl.when(2 * dp >= n_dp)
-        def _():
-            pass_right(0, c)
-
     for copy in lat_copies:
         copy.wait_recv()
     latent = latents[...].reshape(total, pd)
+    key_row = lax.broadcasted_iota(jnp.int32, (1, total), 1)
+    for block in range(n_tp):
+        token = block * rows + lax.broadcasted_iota(jnp.int32, (rows, 1), 0)
+        shift = jnp.zeros_like(token) + place_shift[0] * VP
+        for r in range(1, clip_count):
+            shift = jnp.where(token >= place_start[r] * VP, place_shift[r] * VP, shift)
+        picks = jnp.where(token + shift == key_row, 1.0, 0.0).astype(BF16)
+        packed[pl.ds(block * rows, rows), :] = dot32(picks, latent).astype(BF16)
+
+    def pass_far(c):
+        @pl.when(2 * dp < n_dp)
+        def _():
+            pass_left(0, c)
+
+        @pl.when(2 * dp >= n_dp)
+        def _():
+            pass_right(0, c)
+
+    at_end = (dp == 0) | (dp == n_dp - 1)
+
+    @pl.when(jnp.logical_not(at_end))
+    def _():
+        for c in range(3):
+            pass_far(c)
+
+    def last_piece(c):
+        @pl.when(at_end)
+        def _():
+            pass_far(c)
 
     def projected(c):
+        last_piece(c)
         full = jnp.concatenate([line_sum(0, c), add_sec(1, c)], axis=0)
         high = full.astype(BF16)
         low = (full - high.astype(F32)).astype(BF16)
-        both = dot32(latent, jnp.concatenate([high, low], axis=1))
+        both = dot32(packed[...], jnp.concatenate([high, low], axis=1))
         return both[:, :HD] + both[:, HD:]
 
     def normed(value, gain):
@@ -310,24 +335,22 @@
     keys[...] = normed(projected(1), gk_ref[...])
     values[...] = projected(2).astype(BF16)
 
-    key_row = lax.broadcasted_iota(jnp.int32, (1, total), 1)
-    key_clip = clip_at(key_row)
-    key_place = jnp.zeros_like(key_clip)
-    for c in range(clip_count):
-        key_place = jnp.where(key_clip == c, place_of[c], key_place)
-
-    def attend(block):
-        token = block * rows + lax.broadcasted_iota(jnp.int32, (rows, 1), 0)
+    def place_at(token):
         place = jnp.zeros_like(token)
-        shift = jnp.zeros_like(token) + place_shift[0] * VP
         for r in range(1, clip_count):
-            here = token >= place_start[r] * VP
-            place = place + here.astype(jnp.int32)
-            shift = jnp.where(here, place_shift[r] * VP, shift)
-        picks = jnp.where(token + shift == key_row, 1.0, 0.0).astype(BF16)
-        query = dot32(picks, queries[...]).astype(BF16)
+            place = place + (token >= place_start[r] * VP).astype(jnp.int32)
+        return place
+
+    key_place = place_at(key_row)
+
+    def attend(blocks):
+        query = jnp.concatenate(
+            [queries[pl.ds(pl.multiple_of(block * rows, VP), rows), :] for block in blocks], axis=0
+        )
+        offset = lax.broadcasted_iota(jnp.int32, (rows, 1), 0)
+        token = jnp.concatenate([block * rows + offset for block in blocks], axis=0)
         scores = dot_t(query, keys[...])
-        scores = jnp.where(place == key_place, scores, -1e30)
+        scores = jnp.where(place_at(token) == key_place, scores, -1e30)
         highest = jnp.max(scores, axis=-1, keepdims=True)
         expo = jnp.exp((scores - highest) * HD ** (-0.5))
         weight = jnp.sum(expo, axis=-1, keepdims=True)
@@ -337,17 +360,22 @@
         return pl.ds(pl.multiple_of(head * HD, HD), HD)
 
     out_copies = []
-    for d in range(n_tp - 1, 0, -1):
-        peer = tp_peers[d - 1]
-        mixed[d - 1] = attend(peer)
-        copy = pltpu.make_async_remote_copy(
-            src_ref=mixed.at[d - 1], dst_ref=out_ref.at[:, columns(me)],
-            send_sem=out_send.at[d - 1], recv_sem=out_recv.at[d - 1],
-            device_id={"tp": peer}, device_id_type=MESH,
-        )
-        copy.start()
-        out_copies.append(copy)
-    out_ref[:, columns(me)] = attend(me)
+    steps = list(range(n_tp - 1, -1, -1))
+    for group in [steps[k : k + 2] for k in range(0, n_tp, 2)]:
+        result = attend([tp_peers[d - 1] if d else me for d in group])
+        for k, d in enumerate(group):
+            block_out = result[k * rows : (k + 1) * rows]
+            if d == 0:
+                out_ref[:, columns(me)] = block_out
+                continue
+            mixed[d - 1] = block_out
+            copy = pltpu.make_async_remote_copy(
+                src_ref=mixed.at[d - 1], dst_ref=out_ref.at[:, columns(me)],
+                send_sem=out_send.at[d - 1], recv_sem=out_recv.at[d - 1],
+                device_id={"tp": tp_peers[d - 1]}, device_id_type=MESH,
+            )
+            copy.start()
+            out_copies.append(copy)
 
     for copy in lat_copies:
         copy.wait_send()
@@ -388,16 +416,14 @@
     if not direct_embed:
         slot = lax.axis_index("sec") * n_dp + lax.axis_index("dp")
         embed_weight = lax.dynamic_slice_in_dim(embed_weight, slot * depth, depth, 1)
-    hbm, vmem, smem = (
-        pl.BlockSpec(memory_space=space) for space in (pl.ANY, pltpu.VMEM, pltpu.SMEM)
-    )
+    hbm, vmem = (pl.BlockSpec(memory_space=space) for space in (pl.ANY, pltpu.VMEM))
     dma = pltpu.SemaphoreType.DMA
     sec_links, tp_links = max(1, n_sec - 1), max(1, n_tp - 1)
     pieces = (2, 3, pd // 2, HD)
     out = pl.pallas_call(
         functools.partial(kernel, sizes, direct_embed),
         out_shape=pltpu.VMEM((rows, n_tp * HD), BF16),
-        in_specs=[smem, smem, hbm, hbm, hbm, hbm, hbm, hbm, vmem, vmem],
+        in_specs=[hbm] * 10,
         out_specs=vmem,
         scratch_shapes=[
             pltpu.VMEM(((taps - 1) * VP + rows, fin), BF16),
@@ -412,11 +438,16 @@
             pltpu.VMEM(pieces, BF16),
             pltpu.VMEM(pieces, BF16),
             pltpu.VMEM((n_tp, rows, pd), BF16),
+            pltpu.VMEM((total, pd), BF16),
             pltpu.VMEM((total, HD), BF16),
             pltpu.VMEM((total, HD), BF16),
             pltpu.VMEM((total, HD), BF16),
             pltpu.VMEM((tp_links, rows, HD), BF16),
-            dma((6,)),
+            pltpu.SMEM(frame_clip.shape, jnp.int32),
+            pltpu.SMEM(clip_order.shape, jnp.int32),
+            pltpu.VMEM(q_gain.shape, F32),
+            pltpu.VMEM(k_gain.shape, F32),
+            dma((10,)),
             dma(()),
             dma(()),
             dma((sec_links, 2, 3)),

time: 24 us -> 23 us (0.958)
  Pallas kernels: 23.2 us -> 22.2 us
    pallas_call x1, Pallas kernels: 23.2 us -> 22.2 us  [local(): pl.pallas_call(functools.partial(kernel, sizes, direct_embed), out_shape=...]
where the time goes in v4:
time: 23 us; the launch traced here: 22.9 us
  Pallas kernels  22.2 us (97%)
  local copies, waits for them, and re-layouts  0.66 us (3%)
    pallas_call x1, Pallas kernels, local(): pl.pallas_call(functools.partial(kernel, sizes, direct_embed), out_shape=...  22.2 us
    unnamed x1, local copies, waits for them, and re-layouts  0.66 us

profile of v4, /device:TPU:0, one launch (start us, length us, event | category | flops | bytes accessed | tf_op | source)
XLA Modules:
  0.0 22.9 jit_solution(8514735492736803975)
XLA Ops:
  0.0 22.2 %shard_map.100 = bf16[128,512]{1,0:T(8,128)(2,1)S(1)} custom-call(s32[1,32]{1,0:T(1,128)} %frame_from.1, s32[1,4]{1,0:T(1,128)} %order_from.1, bf16[128,512]{1,0:T(8,128)(2,1)} %bitcast.5, bf16[3,192,512]{2,1,0:T(8,128)(2,1)} %bitcast.4, bf16[192,3072]{1,0:T(8,128)(2,1)} %embed_ref.1, bf16[384,128]{1,0:T(8,128)(2,1)} %wq_ref.1, bf16[384,128]{1,0:T(8,128)(2,1)} %wk_ref.1, ...), custom_call_target="tpu_custom_call" | custom-call | tf_op jit(solution)/shard_map/pallas_call | solution.py:423
  22.2 0.7 %copy.12 = bf16[1,128,512]{2,1,0:T(8,128)(2,1)} copy(bf16[1,128,512]{2,1,0:T(8,128)(2,1)S(1)} %bitcast.3) | data formatting | bytes 262144
